TPU v7x, 128 devices: a whole 4x4x4 slice. The times are simulated.
128 devices in a mesh: depth: 8 (over x, z_hi), screen: 16 (over z_lo, y, core).
Axes of the slice: x: 4, y: 4, z: 4 (z_hi: 2, z_lo: 2; z = z_hi * 2 + z_lo), core: 2. Of those that a mesh axis runs over, the one named last changes fastest.
Arguments:
- voxel_bins: int32 [64, 256, 4096], P('depth', None, 'screen'), may hold values from 0 to 255
- colors: bfloat16 [3, 256], replicated, may hold values from 0 to 2
- opacity: bfloat16 [256], replicated, may hold values from 0 to 1
- slab_order: int32 [16, 8], replicated, may hold values from 0 to 7, each once within a row
Outputs:
- image: float32 [4, 256, 4096], P(None, ('depth', 'screen'))
Inputs may be any that keep to these rules, and one draw needn't show every extreme that they name: `slab_order`: every row is a permutation of 0 to 7.
All inputs are finite; a program needn't handle non-finite values.
Results may differ from a plain program's by a relative error of at most 0.0003.
Values sent between devices are 32-bit elements; how exact they have to be, the bound alone decides.
A program may use at most 64 MiB of HBM per device.

v0:
```python
import math
import jax
import jax.numpy as jnp
from jax import lax
from jax.sharding import PartitionSpec as P

low_count = 16
extinction = 3.0


def look_up(table_rows, bin_block):
    high_count = table_rows.shape[0] // 4
    low_part = bin_block % low_count
    high_part = bin_block // low_count
    low_onehot = (low_part[None, :] == jnp.arange(low_count, dtype=jnp.int32)[:, None]).astype(
        jnp.bfloat16
    )
    picked = jnp.dot(table_rows, low_onehot, preferred_element_type=jnp.float32)
    picked = picked.reshape(4, high_count, bin_block.shape[0])
    high_match = high_part[None, :] == jnp.arange(high_count, dtype=jnp.int32)[:, None]
    return jnp.sum(jnp.where(high_match[None], picked, 0.0), axis=1)


def render(voxel_bins, table_rows, total_samples):
    samples_here, row_count, col_count = voxel_bins.shape
    pixels = row_count * col_count
    per_step = math.gcd(samples_here, max(1, 131072 // pixels))
    blocks = voxel_bins.reshape(samples_here // per_step, per_step * pixels)
    extinct_rate = extinction / total_samples

    def advance(carried, bin_block):
        passed, color_sum = carried
        values = look_up(table_rows, bin_block).reshape(4, per_step, pixels)
        density = values[3]
        before = jnp.cumsum(density, axis=0) - density
        weight = (1.0 - jnp.exp(-extinct_rate * density)) * jnp.exp(
            -extinct_rate * (passed[None] + before)
        )
        color_sum = color_sum + jnp.sum(weight[None] * values[:3], axis=1)
        return ((passed + jnp.sum(density, axis=0), color_sum), None)

    start = (jnp.zeros((pixels,), jnp.float32), jnp.zeros((3, pixels), jnp.float32))
    (passed, color_sum), ignored = lax.scan(advance, start, blocks)
    final_alpha = 1.0 - jnp.exp(-extinct_rate * passed)
    partial_value = jnp.concatenate([color_sum, final_alpha[None]], axis=0)
    return partial_value.reshape(4, row_count, col_count)


def composite(pieces, places):
    in_front = (places[:, None, :] < places[:, :, None]).astype(jnp.float32)
    clear_log = jnp.log1p(-pieces[:, :, 3])
    front_log = jnp.einsum("tij,jtrw->itrw", in_front, clear_log, precision=lax.Precision.HIGHEST)
    shaded = jnp.sum(pieces[:, :, :3] * jnp.exp(front_log)[:, :, None], axis=0)
    total_alpha = 1.0 - jnp.exp(jnp.sum(clear_log, axis=0))
    merged = jnp.concatenate([shaded, total_alpha[:, None]], axis=1)
    return jnp.transpose(merged, (1, 2, 0, 3))


def local(voxel_bins, colors, opacity, slab_order):
    table = jnp.concatenate([colors, opacity[None]], axis=0)
    table_rows = table.reshape(4 * (table.shape[1] // low_count), low_count)
    depth_count = lax.axis_size("depth")
    screen_count = lax.axis_size("screen")
    total_samples = voxel_bins.shape[0] * depth_count
    partial_value = render(voxel_bins, table_rows, total_samples)
    row_count = partial_value.shape[1]
    col_count = partial_value.shape[2]
    owned_rows = row_count // (depth_count * screen_count)
    pieces = lax.all_to_all(
        partial_value[None], ("depth", "screen"), split_axis=2, concat_axis=0, tiled=True
    )
    ordered = pieces.reshape(depth_count, screen_count, 4, pieces.shape[2], pieces.shape[3])
    joined = composite(ordered, slab_order)
    result = joined.reshape(4, owned_rows, screen_count * col_count)
    return result


def solution(mesh):
    placed = (P("depth", None, "screen"), P(), P(), P())
    return jax.shard_map(
        local,
        mesh=mesh,
        in_specs=placed,
        out_specs=P(None, ("depth", "screen"), None),
        check_vma=False,
    )
```

profile of v0, /device:TPU:1, one launch (start us, length us, event | category | flops | bytes accessed | tf_op | source)
XLA Modules:
  0.0 180.9 jit_solution(15716639711246271932)
XLA Ops:
  0.0 4.0 %reshape.117 = s32[4,131072]{1,0:T(4,128)} reshape(s32[8,256,256]{2,1,0:T(8,128)} %param.6) | data formatting | bytes 4194304 | tf_op jit(solution)/shard_map/reshape | solution.py:28
  4.2 140.2 %while.15 = (s32[]{:T(128)}, f32[65536]{0:T(1024)}, f32[3,65536]{1,0:T(4,128)}, s32[4,131072]{1,0:T(4,128)}, bf16[64,16]{0,1:T(8,128)(2,1)S(1)}, /*index=5*/s32[]{:T(128)}, f32[]{:T(128)}, s32[]{:T(128)}) while((s32[]{:T(128)}, f32[65536]{0:T(1024)}, f32[3,65536]{1,0:T(4,128)}, s32[4,131072]{1,0:T(4,128)}, ...), condition=%wide.region_5.6_spmd.clone, body=%wide.region_0.5_spmd.clone.sunk | while | flops 293994496 | bytes 31983784 | solution.py:43
  4.2 3.4 %and_select_fusion.4 = (s32[1,131072]{1,0:T(1,128)S(1)}, s32[1,131072]{1,0:T(1,128)S(1)}) fusion(s32[4,131072]{1,0:T(4,128)} %get-tuple-element.186, s32[]{:T(128)} %get-tuple-element.175), kind=kLoop, calls=%fused_computation.5.clone.1 | loop fusion | flops 1441792 | bytes 1572868 | tf_op jit(solution)/shard_map/while/body/eval_jaxpr/jit(remainder)/select_n | solution.py:13
  7.6 3.8 %and_select_fusion.5 = s32[1,131072]{1,0:T(1,128)S(1)} fusion(s32[1,131072]{1,0:T(1,128)S(1)} %get-tuple-element.163, s32[4,131072]{1,0:T(4,128)} %get-tuple-element.186, s32[]{:T(128)} %get-tuple-element.175), kind=kLoop, calls=%fused_computation.6.clone.1 | loop fusion | flops 1572864 | bytes 1572868 | tf_op jit(solution)/shard_map/while/body/eval_jaxpr/jit(floor_divide)/jit(_where)/select_n | solution.py:14
  12.5 11.0 %select_reduce_fusion.2 = f32[4,131072]{1,0:T(4,128)S(1)} fusion(pred[16,131072]{1,0:T(8,128)(4,1)S(1)} %iota_compare_fusion.4, bf16[64,16]{0,1:T(8,128)(2,1)S(1)} %get-tuple-element.187, s32[131072]{0:T(1024)S(1)} %bitcast.42), kind=kOutput, calls=%fused_computation.clone.1 | convolution fusion | flops 286785536 | bytes 4720640 | tf_op jit(solution)/shard_map/while/body/eval_jaxpr/dot_general | solution.py:18
  30.3 2.9 %slice.38 = f32[3,2,65536]{2,1,0:T(2,128)} reshape(f32[3,131072]{1,0:T(4,128)S(1)} %bitcast.40) | data formatting | bytes 3145728 | tf_op jit(solution)/shard_map/while/body/eval_jaxpr/slice | solution.py:39
  33.1 3.9 %multiply_reduce_fusion.2 = f32[3,65536]{1,0:T(4,128)S(1)} fusion(f32[3,2,65536]{2,1,0:T(2,128)} %slice.38, f32[2,65536]{1,0:T(2,128)S(1)} %exponential_multiply_fusion.2), kind=kLoop, calls=%fused_computation.7.clone.1 | loop fusion | flops 589824 | bytes 2883584 | tf_op jit(solution)/shard_map/while/body/eval_jaxpr/reduce_sum | solution.py:39
  38.6 3.4 %and_select_fusion.4 = (s32[1,131072]{1,0:T(1,128)S(1)}, s32[1,131072]{1,0:T(1,128)S(1)}) fusion(s32[4,131072]{1,0:T(4,128)} %get-tuple-element.186, s32[]{:T(128)} %get-tuple-element.175), kind=kLoop, calls=%fused_computation.5.clone.1 | loop fusion | flops 1441792 | bytes 1572868 | tf_op jit(solution)/shard_map/while/body/eval_jaxpr/jit(remainder)/select_n | solution.py:13
  41.9 3.8 %and_select_fusion.5 = s32[1,131072]{1,0:T(1,128)S(1)} fusion(s32[1,131072]{1,0:T(1,128)S(1)} %get-tuple-element.163, s32[4,131072]{1,0:T(4,128)} %get-tuple-element.186, s32[]{:T(128)} %get-tuple-element.175), kind=kLoop, calls=%fused_computation.6.clone.1 | loop fusion | flops 1572864 | bytes 1572868 | tf_op jit(solution)/shard_map/while/body/eval_jaxpr/jit(floor_divide)/jit(_where)/select_n | solution.py:14
  46.8 11.0 %select_reduce_fusion.2 = f32[4,131072]{1,0:T(4,128)S(1)} fusion(pred[16,131072]{1,0:T(8,128)(4,1)S(1)} %iota_compare_fusion.4, bf16[64,16]{0,1:T(8,128)(2,1)S(1)} %get-tuple-element.187, s32[131072]{0:T(1024)S(1)} %bitcast.42), kind=kOutput, calls=%fused_computation.clone.1 | convolution fusion | flops 286785536 | bytes 4720640 | tf_op jit(solution)/shard_map/while/body/eval_jaxpr/dot_general | solution.py:18
  65.6 2.9 %slice.38 = f32[3,2,65536]{2,1,0:T(2,128)} reshape(f32[3,131072]{1,0:T(4,128)S(1)} %bitcast.40) | data formatting | bytes 3145728 | tf_op jit(solution)/shard_map/while/body/eval_jaxpr/slice | solution.py:39
  68.4 3.9 %multiply_reduce_fusion.2 = f32[3,65536]{1,0:T(4,128)S(1)} fusion(f32[3,2,65536]{2,1,0:T(2,128)} %slice.38, f32[2,65536]{1,0:T(2,128)S(1)} %exponential_multiply_fusion.2), kind=kLoop, calls=%fused_computation.7.clone.1 | loop fusion | flops 589824 | bytes 2883584 | tf_op jit(solution)/shard_map/while/body/eval_jaxpr/reduce_sum | solution.py:39
  73.9 3.4 %and_select_fusion.4 = (s32[1,131072]{1,0:T(1,128)S(1)}, s32[1,131072]{1,0:T(1,128)S(1)}) fusion(s32[4,131072]{1,0:T(4,128)} %get-tuple-element.186, s32[]{:T(128)} %get-tuple-element.175), kind=kLoop, calls=%fused_computation.5.clone.1 | loop fusion | flops 1441792 | bytes 1572868 | tf_op jit(solution)/shard_map/while/body/eval_jaxpr/jit(remainder)/select_n | solution.py:13
  77.2 3.8 %and_select_fusion.5 = s32[1,131072]{1,0:T(1,128)S(1)} fusion(s32[1,131072]{1,0:T(1,128)S(1)} %get-tuple-element.163, s32[4,131072]{1,0:T(4,128)} %get-tuple-element.186, s32[]{:T(128)} %get-tuple-element.175), kind=kLoop, calls=%fused_computation.6.clone.1 | loop fusion | flops 1572864 | bytes 1572868 | tf_op jit(solution)/shard_map/while/body/eval_jaxpr/jit(floor_divide)/jit(_where)/select_n | solution.py:14
  82.1 11.0 %select_reduce_fusion.2 = f32[4,131072]{1,0:T(4,128)S(1)} fusion(pred[16,131072]{1,0:T(8,128)(4,1)S(1)} %iota_compare_fusion.4, bf16[64,16]{0,1:T(8,128)(2,1)S(1)} %get-tuple-element.187, s32[131072]{0:T(1024)S(1)} %bitcast.42), kind=kOutput, calls=%fused_computation.clone.1 | convolution fusion | flops 286785536 | bytes 4720640 | tf_op jit(solution)/shard_map/while/body/eval_jaxpr/dot_general | solution.py:18
  100.8 2.9 %slice.38 = f32[3,2,65536]{2,1,0:T(2,128)} reshape(f32[3,131072]{1,0:T(4,128)S(1)} %bitcast.40) | data formatting | bytes 3145728 | tf_op jit(solution)/shard_map/while/body/eval_jaxpr/slice | solution.py:39
  103.7 3.9 %multiply_reduce_fusion.2 = f32[3,65536]{1,0:T(4,128)S(1)} fusion(f32[3,2,65536]{2,1,0:T(2,128)} %slice.38, f32[2,65536]{1,0:T(2,128)S(1)} %exponential_multiply_fusion.2), kind=kLoop, calls=%fused_computation.7.clone.1 | loop fusion | flops 589824 | bytes 2883584 | tf_op jit(solution)/shard_map/while/body/eval_jaxpr/reduce_sum | solution.py:39
  109.1 3.4 %and_select_fusion.4 = (s32[1,131072]{1,0:T(1,128)S(1)}, s32[1,131072]{1,0:T(1,128)S(1)}) fusion(s32[4,131072]{1,0:T(4,128)} %get-tuple-element.186, s32[]{:T(128)} %get-tuple-element.175), kind=kLoop, calls=%fused_computation.5.clone.1 | loop fusion | flops 1441792 | bytes 1572868 | tf_op jit(solution)/shard_map/while/body/eval_jaxpr/jit(remainder)/select_n | solution.py:13
  112.5 3.8 %and_select_fusion.5 = s32[1,131072]{1,0:T(1,128)S(1)} fusion(s32[1,131072]{1,0:T(1,128)S(1)} %get-tuple-element.163, s32[4,131072]{1,0:T(4,128)} %get-tuple-element.186, s32[]{:T(128)} %get-tuple-element.175), kind=kLoop, calls=%fused_computation.6.clone.1 | loop fusion | flops 1572864 | bytes 1572868 | tf_op jit(solution)/shard_map/while/body/eval_jaxpr/jit(floor_divide)/jit(_where)/select_n | solution.py:14
  117.4 11.0 %select_reduce_fusion.2 = f32[4,131072]{1,0:T(4,128)S(1)} fusion(pred[16,131072]{1,0:T(8,128)(4,1)S(1)} %iota_compare_fusion.4, bf16[64,16]{0,1:T(8,128)(2,1)S(1)} %get-tuple-element.187, s32[131072]{0:T(1024)S(1)} %bitcast.42), kind=kOutput, calls=%fused_computation.clone.1 | convolution fusion | flops 286785536 | bytes 4720640 | tf_op jit(solution)/shard_map/while/body/eval_jaxpr/dot_general | solution.py:18
  136.1 2.9 %slice.38 = f32[3,2,65536]{2,1,0:T(2,128)} reshape(f32[3,131072]{1,0:T(4,128)S(1)} %bitcast.40) | data formatting | bytes 3145728 | tf_op jit(solution)/shard_map/while/body/eval_jaxpr/slice | solution.py:39
  139.0 3.9 %multiply_reduce_fusion.2 = f32[3,65536]{1,0:T(4,128)S(1)} fusion(f32[3,2,65536]{2,1,0:T(2,128)} %slice.38, f32[2,65536]{1,0:T(2,128)S(1)} %exponential_multiply_fusion.2), kind=kLoop, calls=%fused_computation.7.clone.1 | loop fusion | flops 589824 | bytes 2883584 | tf_op jit(solution)/shard_map/while/body/eval_jaxpr/reduce_sum | solution.py:39
  148.1 11.5 %all-to-all-start = ((f32[1,4,256,256]{3,1,0,2:T(4,128)}), f32[1,4,256,256]{3,1,0,2:T(4,128)S(1)}, u32[]{:S(2)}, u32[]{:S(2)}) async-start(f32[1,4,256,256]{3,1,0,2:T(4,128)} %pad_maximum_fusion), calls=%async_computation | async-start | bytes 2097152 | tf_op jit(solution)/shard_map/all_to_all | solution.py:69
  159.7 18.9 %all-to-all-done = f32[1,4,256,256]{3,1,0,2:T(4,128)S(1)} async-done(((f32[1,4,256,256]{3,1,0,2:T(4,128)}), f32[1,4,256,256]{3,1,0,2:T(4,128)S(1)}, u32[]{:S(2)}, u32[]{:S(2)}) %all-to-all-start) | async-done | bytes 1048608 | tf_op jit(solution)/shard_map/all_to_all | solution.py:69
  (73 shorter events, 46.8 us)
Async XLA Ops:
  0.0 4.0 %copy-start.4 = (bf16[256]{0:T(256)(128)(2,1)S(1)}, bf16[256]{0:T(256)(128)(2,1)}, u32[]{:S(2)}) copy-start(bf16[256]{0:T(256)(128)(2,1)} %param.8) | copy-start | bytes 1540
  0.0 4.0 %copy-start.3 = (bf16[3,256]{1,0:T(4,128)(2,1)S(1)}, bf16[3,256]{1,0:T(4,128)(2,1)}, u32[]{:S(2)}) copy-start(bf16[3,256]{1,0:T(4,128)(2,1)} %param.7) | copy-start | bytes 4612
  33.1 3.9 %copy-start = (f32[3,65536]{1,0:T(4,128)S(1)}, f32[3,65536]{1,0:T(4,128)}, u32[]{:S(2)}) copy-start(f32[3,65536]{1,0:T(4,128)} %get-tuple-element.177) | copy-start | bytes 2359300 | tf_op jit(solution)/shard_map/while
  37.6 1.0 copy-start.1
  68.4 3.9 %copy-start = (f32[3,65536]{1,0:T(4,128)S(1)}, f32[3,65536]{1,0:T(4,128)}, u32[]{:S(2)}) copy-start(f32[3,65536]{1,0:T(4,128)} %get-tuple-element.177) | copy-start | bytes 2359300 | tf_op jit(solution)/shard_map/while
  72.9 1.0 copy-start.1
  103.7 3.9 %copy-start = (f32[3,65536]{1,0:T(4,128)S(1)}, f32[3,65536]{1,0:T(4,128)}, u32[]{:S(2)}) copy-start(f32[3,65536]{1,0:T(4,128)} %get-tuple-element.177) | copy-start | bytes 2359300 | tf_op jit(solution)/shard_map/while
  108.2 1.0 copy-start.1
  139.0 3.9 %copy-start = (f32[3,65536]{1,0:T(4,128)S(1)}, f32[3,65536]{1,0:T(4,128)}, u32[]{:S(2)}) copy-start(f32[3,65536]{1,0:T(4,128)} %get-tuple-element.177) | copy-start | bytes 2359300 | tf_op jit(solution)/shard_map/while
  143.5 1.0 copy-start.1
  145.4 14.2 %copy-start.2 = (s32[16,8]{0,1:T(8,128)S(1)}, s32[16,8]{0,1:T(8,128)}, u32[]{:S(2)}) copy-start(s32[16,8]{0,1:T(8,128)} %param.9) | copy-start | bytes 1540
  148.1 30.5 %all-to-all-start = ((f32[1,4,256,256]{3,1,0,2:T(4,128)}), f32[1,4,256,256]{3,1,0,2:T(4,128)S(1)}, u32[]{:S(2)}, u32[]{:S(2)}) async-start(f32[1,4,256,256]{3,1,0,2:T(4,128)} %pad_maximum_fusion), calls=%async_computation | async-start | bytes 2097152 | tf_op jit(solution)/shard_map/all_to_all | solution.py:69
where the time goes:
time: 182 us; the launch traced here: 181 us
  other arithmetic  77.5 us (43%)
  matrix products  44.4 us (24%)
  local copies, waits for them, and re-layouts  28.1 us (15%)
  waiting for transfers between devices  18.9 us (10%)
  starting transfers between devices  11.5 us (6%)
    dot_general x4, matrix products, look_up(): picked = jnp.dot(table_rows, low_onehot, preferred_element_type=jnp.float32)  44 us
    all_to_all x1, waiting for transfers between devices, local(): lax.all_to_all(partial_value[None], ('depth', 'screen'), split_axis=2, co...  18.9 us
    reduce_sum x4, other arithmetic, advance(): color_sum = color_sum + jnp.sum(weight[None] * values[:3], axis=1)  15.4 us
    select_n x4, other arithmetic, look_up(): high_part = bin_block // low_count  15 us
    select_n x4, other arithmetic, look_up(): low_part = bin_block % low_count  13.5 us
    all_to_all x1, starting transfers between devices, local(): lax.all_to_all(partial_value[None], ('depth', 'screen'), split_axis=2, co...  11.5 us
    slice x4, local copies, waits for them, and re-layouts, advance(): color_sum = color_sum + jnp.sum(weight[None] * values[:3], axis=1)  11.4 us
    another operation x4, other arithmetic, advance(): before = jnp.cumsum(density, axis=0) - density  7.29 us
  transfers between devices with their start and end apart: 1, of which 1 were waited for; matrix products, arithmetic and copies ran while one was open for 0% of the time, Pallas kernels for 0%

commit v1 on v0

--- a/solution.py
+++ b/solution.py
@@ -66,8 +66,16 @@
     row_count = partial_value.shape[1]
     col_count = partial_value.shape[2]
     owned_rows = row_count // (depth_count * screen_count)
-    pieces = lax.all_to_all(
-        partial_value[None], ("depth", "screen"), split_axis=2, concat_axis=0, tiled=True
+    pieces = jnp.concatenate(
+        lax.all_to_all(
+            jnp.stack(
+                jnp.split(partial_value[None], lax.axis_size(("depth", "screen")), axis=2), axis=0
+            ),
+            axis_name=("depth", "screen"),
+            split_axis=0,
+            concat_axis=0,
+        ),
+        axis=0,
     )
     ordered = pieces.reshape(depth_count, screen_count, 4, pieces.shape[2], pieces.shape[3])
     joined = composite(ordered, slab_order)

time: 182 us -> 257 us (1.41)
  local copies, waits for them, and re-layouts: 28.1 us -> 106 us
  other arithmetic: 77.5 us -> 74.8 us
    unnamed x8 -> x136, local copies, waits for them, and re-layouts: 0.16 us -> 77.4 us
    concatenate x1 -> x0, other arithmetic: 2.72 us -> none  [render(): partial_value = jnp.concatenate([color_sum, final_alpha[None]], axis=0)]
where the time goes in v1:
time: 257 us; the launch traced here: 256 us
  local copies, waits for them, and re-layouts  106 us (41%)
  other arithmetic  74.8 us (29%)
  matrix products  44.5 us (17%)
  waiting for transfers between devices  18.9 us (7%)
  starting transfers between devices  11.5 us (4%)
    unnamed x136, local copies, waits for them, and re-layouts  77.4 us
    dot_general x4, matrix products, look_up(): picked = jnp.dot(table_rows, low_onehot, preferred_element_type=jnp.float32)  44 us
    all_to_all x1, waiting for transfers between devices, local(): lax.all_to_all(jnp.stack(jnp.split(partial_value[None], lax.axis_size(('d...  18.9 us
    reduce_sum x4, other arithmetic, advance(): color_sum = color_sum + jnp.sum(weight[None] * values[:3], axis=1)  15.4 us
    select_n x4, other arithmetic, look_up(): high_part = bin_block // low_count  15 us
    select_n x4, other arithmetic, look_up(): low_part = bin_block % low_count  13.5 us
    all_to_all x1, starting transfers between devices, local(): lax.all_to_all(jnp.stack(jnp.split(partial_value[None], lax.axis_size(('d...  11.5 us
    slice x4, local copies, waits for them, and re-layouts, advance(): color_sum = color_sum + jnp.sum(weight[None] * values[:3], axis=1)  11.4 us
  transfers between devices with their start and end apart: 1, of which 1 were waited for; matrix products, arithmetic and copies ran while one was open for 0% of the time, Pallas kernels for 0%

profile of v1, /device:TPU:1, one launch (start us, length us, event | category | flops | bytes accessed | tf_op | source)
XLA Modules:
  0.0 256.2 jit_solution(15444917599498797046)
XLA Ops:
  0.0 4.0 %reshape.113 = s32[4,131072]{1,0:T(4,128)} reshape(s32[8,256,256]{2,1,0:T(8,128)} %param.6) | data formatting | bytes 4194304 | tf_op jit(solution)/shard_map/reshape | solution.py:28
  4.2 140.2 %while.15 = (s32[]{:T(128)}, f32[65536]{0:T(1024)}, f32[3,65536]{1,0:T(4,128)}, s32[4,131072]{1,0:T(4,128)}, bf16[64,16]{0,1:T(8,128)(2,1)S(1)}, /*index=5*/s32[]{:T(128)}, f32[]{:T(128)}, s32[]{:T(128)}) while((s32[]{:T(128)}, f32[65536]{0:T(1024)}, f32[3,65536]{1,0:T(4,128)}, s32[4,131072]{1,0:T(4,128)}, ...), condition=%wide.region_5.6_spmd.clone, body=%wide.region_0.5_spmd.clone.sunk | while | flops 293994496 | bytes 31983784 | solution.py:43
  4.2 3.4 %and_select_fusion.4 = (s32[1,131072]{1,0:T(1,128)S(1)}, s32[1,131072]{1,0:T(1,128)S(1)}) fusion(s32[4,131072]{1,0:T(4,128)} %get-tuple-element.181, s32[]{:T(128)} %get-tuple-element.170), kind=kLoop, calls=%fused_computation.5.clone.1 | loop fusion | flops 1441792 | bytes 1572868 | tf_op jit(solution)/shard_map/while/body/eval_jaxpr/jit(remainder)/select_n | solution.py:13
  7.6 3.8 %and_select_fusion.5 = s32[1,131072]{1,0:T(1,128)S(1)} fusion(s32[1,131072]{1,0:T(1,128)S(1)} %get-tuple-element.158, s32[4,131072]{1,0:T(4,128)} %get-tuple-element.181, s32[]{:T(128)} %get-tuple-element.170), kind=kLoop, calls=%fused_computation.6.clone.1 | loop fusion | flops 1572864 | bytes 1572868 | tf_op jit(solution)/shard_map/while/body/eval_jaxpr/jit(floor_divide)/jit(_where)/select_n | solution.py:14
  12.5 11.0 %select_reduce_fusion.2 = f32[4,131072]{1,0:T(4,128)S(1)} fusion(pred[16,131072]{1,0:T(8,128)(4,1)S(1)} %iota_compare_fusion.4, bf16[64,16]{0,1:T(8,128)(2,1)S(1)} %get-tuple-element.182, s32[131072]{0:T(1024)S(1)} %bitcast.553), kind=kOutput, calls=%fused_computation.clone.1 | convolution fusion | flops 286785536 | bytes 4720640 | tf_op jit(solution)/shard_map/while/body/eval_jaxpr/dot_general | solution.py:18
  30.3 2.9 %slice.38 = f32[3,2,65536]{2,1,0:T(2,128)} reshape(f32[3,131072]{1,0:T(4,128)S(1)} %bitcast.551) | data formatting | bytes 3145728 | tf_op jit(solution)/shard_map/while/body/eval_jaxpr/slice | solution.py:39
  33.1 3.9 %multiply_reduce_fusion.2 = f32[3,65536]{1,0:T(4,128)S(1)} fusion(f32[3,2,65536]{2,1,0:T(2,128)} %slice.38, f32[2,65536]{1,0:T(2,128)S(1)} %exponential_multiply_fusion.2), kind=kLoop, calls=%fused_computation.7.clone.1 | loop fusion | flops 589824 | bytes 2883584 | tf_op jit(solution)/shard_map/while/body/eval_jaxpr/reduce_sum | solution.py:39
  38.6 3.4 %and_select_fusion.4 = (s32[1,131072]{1,0:T(1,128)S(1)}, s32[1,131072]{1,0:T(1,128)S(1)}) fusion(s32[4,131072]{1,0:T(4,128)} %get-tuple-element.181, s32[]{:T(128)} %get-tuple-element.170), kind=kLoop, calls=%fused_computation.5.clone.1 | loop fusion | flops 1441792 | bytes 1572868 | tf_op jit(solution)/shard_map/while/body/eval_jaxpr/jit(remainder)/select_n | solution.py:13
  41.9 3.8 %and_select_fusion.5 = s32[1,131072]{1,0:T(1,128)S(1)} fusion(s32[1,131072]{1,0:T(1,128)S(1)} %get-tuple-element.158, s32[4,131072]{1,0:T(4,128)} %get-tuple-element.181, s32[]{:T(128)} %get-tuple-element.170), kind=kLoop, calls=%fused_computation.6.clone.1 | loop fusion | flops 1572864 | bytes 1572868 | tf_op jit(solution)/shard_map/while/body/eval_jaxpr/jit(floor_divide)/jit(_where)/select_n | solution.py:14
  46.8 11.0 %select_reduce_fusion.2 = f32[4,131072]{1,0:T(4,128)S(1)} fusion(pred[16,131072]{1,0:T(8,128)(4,1)S(1)} %iota_compare_fusion.4, bf16[64,16]{0,1:T(8,128)(2,1)S(1)} %get-tuple-element.182, s32[131072]{0:T(1024)S(1)} %bitcast.553), kind=kOutput, calls=%fused_computation.clone.1 | convolution fusion | flops 286785536 | bytes 4720640 | tf_op jit(solution)/shard_map/while/body/eval_jaxpr/dot_general | solution.py:18
  65.6 2.9 %slice.38 = f32[3,2,65536]{2,1,0:T(2,128)} reshape(f32[3,131072]{1,0:T(4,128)S(1)} %bitcast.551) | data formatting | bytes 3145728 | tf_op jit(solution)/shard_map/while/body/eval_jaxpr/slice | solution.py:39
  68.4 3.9 %multiply_reduce_fusion.2 = f32[3,65536]{1,0:T(4,128)S(1)} fusion(f32[3,2,65536]{2,1,0:T(2,128)} %slice.38, f32[2,65536]{1,0:T(2,128)S(1)} %exponential_multiply_fusion.2), kind=kLoop, calls=%fused_computation.7.clone.1 | loop fusion | flops 589824 | bytes 2883584 | tf_op jit(solution)/shard_map/while/body/eval_jaxpr/reduce_sum | solution.py:39
  73.9 3.4 %and_select_fusion.4 = (s32[1,131072]{1,0:T(1,128)S(1)}, s32[1,131072]{1,0:T(1,128)S(1)}) fusion(s32[4,131072]{1,0:T(4,128)} %get-tuple-element.181, s32[]{:T(128)} %get-tuple-element.170), kind=kLoop, calls=%fused_computation.5.clone.1 | loop fusion | flops 1441792 | bytes 1572868 | tf_op jit(solution)/shard_map/while/body/eval_jaxpr/jit(remainder)/select_n | solution.py:13
  77.2 3.8 %and_select_fusion.5 = s32[1,131072]{1,0:T(1,128)S(1)} fusion(s32[1,131072]{1,0:T(1,128)S(1)} %get-tuple-element.158, s32[4,131072]{1,0:T(4,128)} %get-tuple-element.181, s32[]{:T(128)} %get-tuple-element.170), kind=kLoop, calls=%fused_computation.6.clone.1 | loop fusion | flops 1572864 | bytes 1572868 | tf_op jit(solution)/shard_map/while/body/eval_jaxpr/jit(floor_divide)/jit(_where)/select_n | solution.py:14
  82.1 11.0 %select_reduce_fusion.2 = f32[4,131072]{1,0:T(4,128)S(1)} fusion(pred[16,131072]{1,0:T(8,128)(4,1)S(1)} %iota_compare_fusion.4, bf16[64,16]{0,1:T(8,128)(2,1)S(1)} %get-tuple-element.182, s32[131072]{0:T(1024)S(1)} %bitcast.553), kind=kOutput, calls=%fused_computation.clone.1 | convolution fusion | flops 286785536 | bytes 4720640 | tf_op jit(solution)/shard_map/while/body/eval_jaxpr/dot_general | solution.py:18
  100.8 2.9 %slice.38 = f32[3,2,65536]{2,1,0:T(2,128)} reshape(f32[3,131072]{1,0:T(4,128)S(1)} %bitcast.551) | data formatting | bytes 3145728 | tf_op jit(solution)/shard_map/while/body/eval_jaxpr/slice | solution.py:39
  103.7 3.9 %multiply_reduce_fusion.2 = f32[3,65536]{1,0:T(4,128)S(1)} fusion(f32[3,2,65536]{2,1,0:T(2,128)} %slice.38, f32[2,65536]{1,0:T(2,128)S(1)} %exponential_multiply_fusion.2), kind=kLoop, calls=%fused_computation.7.clone.1 | loop fusion | flops 589824 | bytes 2883584 | tf_op jit(solution)/shard_map/while/body/eval_jaxpr/reduce_sum | solution.py:39
  109.1 3.4 %and_select_fusion.4 = (s32[1,131072]{1,0:T(1,128)S(1)}, s32[1,131072]{1,0:T(1,128)S(1)}) fusion(s32[4,131072]{1,0:T(4,128)} %get-tuple-element.181, s32[]{:T(128)} %get-tuple-element.170), kind=kLoop, calls=%fused_computation.5.clone.1 | loop fusion | flops 1441792 | bytes 1572868 | tf_op jit(solution)/shard_map/while/body/eval_jaxpr/jit(remainder)/select_n | solution.py:13
  112.5 3.8 %and_select_fusion.5 = s32[1,131072]{1,0:T(1,128)S(1)} fusion(s32[1,131072]{1,0:T(1,128)S(1)} %get-tuple-element.158, s32[4,131072]{1,0:T(4,128)} %get-tuple-element.181, s32[]{:T(128)} %get-tuple-element.170), kind=kLoop, calls=%fused_computation.6.clone.1 | loop fusion | flops 1572864 | bytes 1572868 | tf_op jit(solution)/shard_map/while/body/eval_jaxpr/jit(floor_divide)/jit(_where)/select_n | solution.py:14
  117.4 11.0 %select_reduce_fusion.2 = f32[4,131072]{1,0:T(4,128)S(1)} fusion(pred[16,131072]{1,0:T(8,128)(4,1)S(1)} %iota_compare_fusion.4, bf16[64,16]{0,1:T(8,128)(2,1)S(1)} %get-tuple-element.182, s32[131072]{0:T(1024)S(1)} %bitcast.553), kind=kOutput, calls=%fused_computation.clone.1 | convolution fusion | flops 286785536 | bytes 4720640 | tf_op jit(solution)/shard_map/while/body/eval_jaxpr/dot_general | solution.py:18
  136.1 2.9 %slice.38 = f32[3,2,65536]{2,1,0:T(2,128)} reshape(f32[3,131072]{1,0:T(4,128)S(1)} %bitcast.551) | data formatting | bytes 3145728 | tf_op jit(solution)/shard_map/while/body/eval_jaxpr/slice | solution.py:39
  139.0 3.9 %multiply_reduce_fusion.2 = f32[3,65536]{1,0:T(4,128)S(1)} fusion(f32[3,2,65536]{2,1,0:T(2,128)} %slice.38, f32[2,65536]{1,0:T(2,128)S(1)} %exponential_multiply_fusion.2), kind=kLoop, calls=%fused_computation.7.clone.1 | loop fusion | flops 589824 | bytes 2883584 | tf_op jit(solution)/shard_map/while/body/eval_jaxpr/reduce_sum | solution.py:39
  223.5 11.5 %all-to-all-start = ((f32[128,1,4,2,256]{4,3,2,1,0:T(2,128)}), f32[128,1,4,2,256]{4,3,2,1,0:T(2,128)S(1)}, u32[]{:S(2)}, u32[]{:S(2)}) async-start(f32[128,1,4,2,256]{4,3,2,1,0:T(2,128)} %constant_dynamic-update-slice_fusion.1), calls=%async_computation | async-start | bytes 2097152 | tf_op jit(solution)/shard_map/all_to_all | solution.py:70
  235.1 18.9 %all-to-all-done = f32[128,1,4,2,256]{4,3,2,1,0:T(2,128)S(1)} async-done(((f32[128,1,4,2,256]{4,3,2,1,0:T(2,128)}), f32[128,1,4,2,256]{4,3,2,1,0:T(2,128)S(1)}, u32[]{:S(2)}, u32[]{:S(2)}) %all-to-all-start) | async-done | bytes 1048608 | tf_op jit(solution)/shard_map/all_to_all | solution.py:70
  (203 shorter events, 122.0 us)
Async XLA Ops:
  0.0 4.0 %copy-start.4 = (bf16[256]{0:T(256)(128)(2,1)S(1)}, bf16[256]{0:T(256)(128)(2,1)}, u32[]{:S(2)}) copy-start(bf16[256]{0:T(256)(128)(2,1)} %param.8) | copy-start | bytes 1540
  0.0 4.0 %copy-start.3 = (bf16[3,256]{1,0:T(4,128)(2,1)S(1)}, bf16[3,256]{1,0:T(4,128)(2,1)}, u32[]{:S(2)}) copy-start(bf16[3,256]{1,0:T(4,128)(2,1)} %param.7) | copy-start | bytes 4612
  33.1 3.9 %copy-start = (f32[3,65536]{1,0:T(4,128)S(1)}, f32[3,65536]{1,0:T(4,128)}, u32[]{:S(2)}) copy-start(f32[3,65536]{1,0:T(4,128)} %get-tuple-element.172) | copy-start | bytes 2359300 | tf_op jit(solution)/shard_map/while
  37.6 1.0 copy-start.1
  68.4 3.9 %copy-start = (f32[3,65536]{1,0:T(4,128)S(1)}, f32[3,65536]{1,0:T(4,128)}, u32[]{:S(2)}) copy-start(f32[3,65536]{1,0:T(4,128)} %get-tuple-element.172) | copy-start | bytes 2359300 | tf_op jit(solution)/shard_map/while
  72.9 1.0 copy-start.1
  103.7 3.9 %copy-start = (f32[3,65536]{1,0:T(4,128)S(1)}, f32[3,65536]{1,0:T(4,128)}, u32[]{:S(2)}) copy-start(f32[3,65536]{1,0:T(4,128)} %get-tuple-element.172) | copy-start | bytes 2359300 | tf_op jit(solution)/shard_map/while
  108.2 1.0 copy-start.1
  139.0 3.9 %copy-start = (f32[3,65536]{1,0:T(4,128)S(1)}, f32[3,65536]{1,0:T(4,128)}, u32[]{:S(2)}) copy-start(f32[3,65536]{1,0:T(4,128)} %get-tuple-element.172) | copy-start | bytes 2359300 | tf_op jit(solution)/shard_map/while
  143.5 1.0 copy-start.1
  146.9 88.1 %copy-start.2 = (s32[16,8]{0,1:T(8,128)S(1)}, s32[16,8]{0,1:T(8,128)}, u32[]{:S(2)}) copy-start(s32[16,8]{0,1:T(8,128)} %param.9) | copy-start | bytes 1540
  223.5 30.5 %all-to-all-start = ((f32[128,1,4,2,256]{4,3,2,1,0:T(2,128)}), f32[128,1,4,2,256]{4,3,2,1,0:T(2,128)S(1)}, u32[]{:S(2)}, u32[]{:S(2)}) async-start(f32[128,1,4,2,256]{4,3,2,1,0:T(2,128)} %constant_dynamic-update-slice_fusion.1), calls=%async_computation | async-start | bytes 2097152 | tf_op jit(solution)/shard_map/all_to_all | solution.py:70
